TPU v7x, 32 devices: a whole 2x2x4 slice. The times are simulated.
32 devices in a mesh: tile: 8 (over z, x), mem: 4 (over y, core).
Axes of the slice: x: 2, y: 2, z: 4, core: 2. Of those that a mesh axis runs over, the one named last changes fastest.
Arguments:
- footprints: bfloat16 [1024, 128, 128], P('tile'), may hold values from -0.1875 to 0.1875
- tile_row: int32 [1024], P('tile'), may hold values from 0 to 127, as said below
- tile_col: int32 [1024], P('tile'), may hold values from 0 to 63, as said below
- prior_flux: bfloat16 [256, 8192], P('mem', 'tile'), may hold values from -12 to 12
- observed: float32 [256, 16384], P('mem', 'tile'), may hold values from -6 to 6
- precision_weight: int32 [16384], P('tile'), may hold values from 1 to 16
Outputs:
- gradient: float32 [256, 8192], P('mem', 'tile')
Inputs may be any that keep to these rules, and one draw needn't show every extreme that they name: Among the 128 tiles of each index of tile, at most 24 have a row block of one owner (owner = tile_row // 16); in every draw one owner gets exactly 24 from every index. Likewise with owner = tile_col // 8: at most 24 from one index of tile to one owner, and one owner gets exactly 24 from every index.
All inputs are finite; a program needn't handle non-finite values.
Results may differ from a plain program's by a relative error of at most 0.0052.
Values may be sent and summed in bfloat16 or wider, within the bound.
No kernel may reach another device: no remote copies, remote signals or barrier semaphores. Data moves between devices by JAX's collectives and lax.ppermute only.
A program may use at most 64 MiB of HBM per device.

v0:
```python
import jax
import jax.numpy as jnp
from jax import lax
from jax.sharding import PartitionSpec as P

MEMBERS = 256
FLUX_DEV = 8
SOUND_DEV = 16


def slot_of(owners, capacity):
    entries = owners.shape[0]
    position = jnp.arange(entries)
    earlier = (owners[:, None] == owners[None, :]) & (position[None, :] < position[:, None])
    return owners * capacity + jnp.sum(earlier.astype(jnp.int32), axis=1)


def invert(slot_ids, slot_total):
    matches = slot_ids[None, :] == jnp.arange(slot_total)[:, None]
    sources = jnp.sum(jnp.where(matches, jnp.arange(slot_ids.shape[0])[None, :], 0), axis=1)
    return (sources, jnp.any(matches, axis=1))


def to_slots(values, sources, usage_flags):
    placed = jnp.take(values, sources, axis=1)
    return jnp.where(usage_flags[None, :, None], placed, jnp.zeros_like(placed))


def body(footprints, tile_row, tile_col, prior_flux, observed, precision_weight):
    devices_tile = lax.axis_size("tile")
    tile_count = footprints.shape[0]
    tile_size = footprints.shape[1]
    capacity = tile_count // devices_tile + max(1, tile_count // (2 * devices_tile))
    slot_total = devices_tile * capacity
    local_members = prior_flux.shape[0]
    local_sum = jnp.sum(prior_flux.astype(jnp.float32), axis=0)
    ensemble_sum = lax.psum(local_sum, "mem")
    ensemble_mean = ensemble_sum / MEMBERS
    member_deviations = (prior_flux.astype(jnp.float32) - ensemble_mean[None, :]).astype(
        jnp.bfloat16
    )
    row_owner = tile_row // SOUND_DEV
    row_local = tile_row % SOUND_DEV
    row_slot = slot_of(row_owner, capacity)
    row_source, row_used = invert(row_slot, slot_total)
    gathered = lax.all_gather(member_deviations, "tile", axis=1, tiled=True)
    retrieved_blocks = jnp.take(gathered.reshape(local_members, -1, tile_size), tile_col, axis=1)
    forward_terms = jnp.einsum(
        "mtk,trk->mtr", retrieved_blocks, footprints, preferred_element_type=jnp.float32
    )
    row_index = jnp.where(row_used, jnp.take(row_local, row_source), SOUND_DEV)
    sent_terms = to_slots(forward_terms, row_source, row_used)
    got_terms, got_rows = (
        lax.all_to_all(sent_terms, "tile", split_axis=1, concat_axis=1, tiled=True),
        lax.all_to_all(row_index[None, :], "tile", split_axis=1, concat_axis=1, tiled=True),
    )
    got_rows = got_rows[0]
    row_match = (got_rows[None, :] == jnp.arange(SOUND_DEV)[:, None]).astype(jnp.float32)
    modelled = jnp.einsum("ds,msk->mdk", row_match, got_terms, precision=lax.Precision.HIGHEST)
    targets = observed.reshape(local_members, SOUND_DEV, tile_size)
    obs_weight = (precision_weight.astype(jnp.float32) / 8.0).reshape(SOUND_DEV, tile_size)
    weighted = (obs_weight[None, :, :] * (modelled - targets)).astype(jnp.bfloat16)
    reply_rows = jnp.take(weighted, jnp.minimum(got_rows, SOUND_DEV - 1), axis=1)
    returned = lax.all_to_all(reply_rows, "tile", split_axis=1, concat_axis=1, tiled=True)
    residual_tiles = jnp.take(returned, row_slot, axis=1)
    backward_terms = jnp.einsum(
        "mtr,trk->mtk", residual_tiles, footprints, preferred_element_type=jnp.float32
    )
    picked = (tile_col[None, :] == jnp.arange(lax.axis_size("tile") * FLUX_DEV)[:, None]).astype(
        jnp.float32
    )
    reduced_total = lax.psum_scatter(
        jnp.einsum("ct,mtk->cmk", picked, backward_terms, precision=lax.Precision.HIGHEST),
        "tile",
        scatter_dimension=0,
        tiled=True,
    )
    gradient = reduced_total.transpose(1, 0, 2).reshape(local_members, FLUX_DEV * tile_size)
    return gradient


def solution(mesh):
    in_specs = (
        P("tile", None, None),
        P("tile"),
        P("tile"),
        P("mem", "tile"),
        P("mem", "tile"),
        P("tile"),
    )
    out_specs = P("mem", "tile")
    return jax.shard_map(body, mesh=mesh, in_specs=in_specs, out_specs=out_specs, check_vma=False)
```

profile of v0, /device:TPU:0, one launch (start us, length us, event | category | flops | bytes accessed | tf_op | source)
XLA Modules:
  0.0 394.9 jit_solution(9114734959783431947)
XLA Ops:
  6.5 0.0 all-gather.2.cloned.1.call-start
  6.5 0.9 convert_reduce_fusion
  7.5 8.4 %psum.7 = f32[1024]{0:T(1024)S(1)} all-reduce(f32[1024]{0:T(1024)S(1)} %convert_reduce_fusion), channel_id=1, replica_groups=mesh['tile'=8,'mem'=4] {'mem'}, use_global_device_ids=true, to_apply=%region_4.5 | all-reduce | flops 1024 | bytes 8192 | tf_op jit(solution)/shard_map/psum | solution.py:37
  15.9 1.6 fusion.24
  17.5 0.0 all-gather.2.cloned.1.call-update
  17.5 0.7 and_select_fusion
  18.2 0.2 convert_reduce_fusion.1
  18.4 0.1 select_reduce_fusion
  18.5 0.1 reduce_sum.33
  18.6 1.6 gather_fusion
  20.1 0.1 gather.23
  20.2 0.1 fusion.25
  20.3 0.1 reduce_or.12
  20.4 0.6 select_select_fusion
  21.0 5.8 %all-to-all-start = ((s32[1,8,24]{2,0,1:T(1,128)}), s32[1,8,24]{2,0,1:T(1,128)S(1)}, u32[]{:S(2)}, u32[]{:S(2)}) async-start(s32[1,8,24]{2,0,1:T(1,128)} %bitcast.3), calls=%async_computation | async-start | bytes 8192 | tf_op jit(solution)/shard_map/all_to_all | solution.py:55
  26.8 0.7 compare_select_fusion.5
  27.5 0.7 compare_and_fusion
  28.2 30.0 %all-gather.2.cloned.1.call-done = bf16[64,8192]{1,0:T(8,128)(2,1)} async-done(((bf16[64,1024]{1,0:T(8,128)(2,1)}), bf16[64,8192]{1,0:T(8,128)(2,1)}) %all-gather.2.cloned.1.call-update) | async-done | bytes 1048592 | tf_op jit(solution)/shard_map/all_gather | solution.py:46
  58.2 1.5 copy_bitcast_fusion
  59.7 1.0 gather_fusion.1
  60.7 7.0 %convolution_bitcast_fusion.1 = f32[64,128,128]{2,0,1:T(8,128)} fusion(bf16[128,128,128]{2,1,0:T(8,128)(2,1)} %param.6, bf16[128,64,128]{2,1,0:T(8,128)(2,1)S(1)} %gather_fusion.1, pred[128]{0:T(512)(128)(4,1)S(1)} %compare_and_fusion), kind=kOutput, calls=%fused_computation.12 | convolution fusion | flops 269484032 | bytes 10485888 | tf_op jit(solution)/shard_map/mtk,trk->mtr/dot_general | solution.py:48
  67.7 5.8 %gather_fusion.2 = f32[192,64,128]{2,1,0:T(8,128)} fusion(f32[64,128,128]{2,0,1:T(8,128)} %convolution_bitcast_fusion.1, s32[1024]{0:T(1024)S(1)} %pad_clamp_fusion.3), kind=kCustom, calls=%fused_computation.2 | custom fusion | bytes 12583680 | tf_op jit(solution)/shard_map/jit(_take)/gather | solution.py:25
  73.5 5.4 %select_bitcast_fusion = f32[64,192,128]{2,0,1:T(8,128)} fusion(f32[192,64,128]{2,1,0:T(8,128)} %gather_fusion.2, pred[192]{0:T(512)(128)(4,1)S(1)} %fusion.25, pred[192]{0:T(512)(128)(4,1)S(1)} %compare_and_fusion.1), kind=kLoop, calls=%fused_computation.7 | loop fusion | flops 3145728 | bytes 12583296 | tf_op jit(solution)/shard_map/jit(_where)/select_n | solution.py:26
  79.0 0.0 copy-start
  79.0 0.0 copy-start.1
  79.0 0.0 all-to-all-done
  79.0 4.9 %all-to-all-start.1 = ((f32[64,192,128]{2,0,1:T(8,128)}), f32[64,192,128]{2,0,1:T(8,128)}, u32[]{:S(2)}, u32[]{:S(2)}) async-start(f32[64,192,128]{2,0,1:T(8,128)} %select_bitcast_fusion), calls=%async_computation.1 | async-start | bytes 12582912 | tf_op jit(solution)/shard_map/all_to_all | solution.py:54
  83.9 0.0 copy-done
  83.9 0.1 copy.26
  84.0 0.0 copy-done.1
  84.0 0.5 broadcast.213
  84.5 0.7 minimum_reduce_fusion
  85.2 0.1 squeeze.3
  85.3 0.1 min.26
  85.4 135.2 %all-to-all-done.1 = f32[64,192,128]{2,0,1:T(8,128)} async-done(((f32[64,192,128]{2,0,1:T(8,128)}), f32[64,192,128]{2,0,1:T(8,128)}, u32[]{:S(2)}, u32[]{:S(2)}) %all-to-all-start.1) | async-done | bytes 6291488 | tf_op jit(solution)/shard_map/all_to_all | solution.py:54
  220.6 8.1 %fusion.19 = bf16[64,16,128]{2,1,0:T(8,128)(2,1)S(1)} fusion(f32[64,16,128]{2,1,0:T(8,128)S(1)} %bitcast.49, f32[64,192,128]{2,0,1:T(8,128)} %all-to-all-done.1, f32[16,128]{1,0:T(8,128)S(1)} %multiply_bitcast_fusion, s32[192]{0:T(256)S(1)} %squeeze.3), kind=kOutput, calls=%fused_computation.22 | convolution fusion | flops 302386176 | bytes 7086848 | tf_op jit(solution)/shard_map/ds,msk->mdk/dot_general | solution.py:59
  228.7 0.1 copy.23
  228.7 1.2 gather_fusion.3
  229.9 2.1 select_bitcast_fusion.1
  232.0 3.6 all-to-all-start.2
  235.6 0.0 reduce-scatter.2.cloned.1.call-start
  235.7 70.8 %all-to-all-done.2 = bf16[64,192,128]{2,0,1:T(8,128)(2,1)S(1)} async-done(((bf16[64,192,128]{2,0,1:T(8,128)(2,1)}), bf16[64,192,128]{2,0,1:T(8,128)(2,1)S(1)}, u32[]{:S(2)}, u32[]{:S(2)}) %all-to-all-start.2) | async-done | bytes 3145760 | tf_op jit(solution)/shard_map/all_to_all | solution.py:64
  306.5 2.2 gather_fusion.4
  308.7 0.0 copy-start.2
  308.7 4.1 %convolution_bitcast_fusion = f32[64,128,128]{2,0,1:T(8,128)S(1)} fusion(bf16[128,128,128]{2,1,0:T(8,128)(2,1)} %param.6, bf16[128,64,128]{2,1,0:T(8,128)(2,1)} %gather_fusion.4, pred[128]{0:T(512)(128)(4,1)S(1)} %get-tuple-element.7), kind=kOutput, calls=%fused_computation.11 | convolution fusion | flops 269484032 | bytes 10485888 | tf_op jit(solution)/shard_map/mtr,trk->mtk/dot_general | solution.py:66
  312.8 0.0 copy-done.2
  312.8 5.4 %fusion.2 = f32[64,64,128]{2,0,1:T(8,128)} fusion(f32[64,128,128]{2,0,1:T(8,128)S(1)} %convolution_bitcast_fusion, s32[128]{0:T(128)S(1)} %copy-done.2), kind=kOutput, calls=%fused_computation.8 | convolution fusion | flops 805314560 | bytes 6291968 | tf_op jit(solution)/shard_map/ct,mtk->cmk/dot_general | solution.py:73
  318.2 0.0 reduce-scatter.2.cloned.1.call-update
  318.3 68.2 %reduce-scatter.2.cloned.1.call-done = f32[8,64,128]{2,0,1:T(8,128)} async-done(((f32[64,64,128]{2,0,1:T(8,128)}), f32[8,64,128]{2,0,1:T(8,128)}) %reduce-scatter.2.cloned.1.call-update) | async-done | bytes 262160 | tf_op jit(solution)/shard_map/reduce_scatter | solution.py:72
  386.4 1.7 copy.42
  (12 shorter events, 0.1 us)
Async XLA Ops:
  6.5 51.7 %all-gather.2.cloned.1.call-start = ((), (), s32[]{:S(2)}) async-start(), calls=%async_computation.4 | async-start | bytes 1179648 | tf_op jit(solution)/shard_map/all_gather | solution.py:46
  21.0 57.9 %all-to-all-start = ((s32[1,8,24]{2,0,1:T(1,128)}), s32[1,8,24]{2,0,1:T(1,128)S(1)}, u32[]{:S(2)}, u32[]{:S(2)}) async-start(s32[1,8,24]{2,0,1:T(1,128)} %bitcast.3), calls=%async_computation | async-start | bytes 8192 | tf_op jit(solution)/shard_map/all_to_all | solution.py:55
  79.0 4.9 %copy-start = (f32[64,2048]{1,0:T(8,128)S(1)}, f32[64,2048]{1,0:T(8,128)}, u32[]{:S(2)}) copy-start(f32[64,2048]{1,0:T(8,128)} %param.10) | copy-start | bytes 1572868
  79.0 5.0 %copy-start.1 = (s32[2048]{0:T(1024)S(1)}, s32[2048]{0:T(1024)}, u32[]{:S(2)}) copy-start(s32[2048]{0:T(1024)} %param.11) | copy-start | bytes 24580
  79.0 141.6 %all-to-all-start.1 = ((f32[64,192,128]{2,0,1:T(8,128)}), f32[64,192,128]{2,0,1:T(8,128)}, u32[]{:S(2)}, u32[]{:S(2)}) async-start(f32[64,192,128]{2,0,1:T(8,128)} %select_bitcast_fusion), calls=%async_computation.1 | async-start | bytes 12582912 | tf_op jit(solution)/shard_map/all_to_all | solution.py:54
  232.0 74.5 %all-to-all-start.2 = ((bf16[64,192,128]{2,0,1:T(8,128)(2,1)}), bf16[64,192,128]{2,0,1:T(8,128)(2,1)S(1)}, u32[]{:S(2)}, u32[]{:S(2)}) async-start(bf16[64,192,128]{2,0,1:T(8,128)(2,1)} %select_bitcast_fusion.1), calls=%async_computation.2 | async-start | bytes 6291456 | tf_op jit(solution)/shard_map/all_to_all | solution.py:64
  235.6 150.8 %reduce-scatter.2.cloned.1.call-start = ((), (), s32[]{:S(2)}) async-start(), calls=%async_computation.5 | async-start | bytes 2359296 | tf_op jit(solution)/shard_map/reduce_scatter | solution.py:72
  308.7 4.1 %copy-start.2 = (s32[128]{0:T(128)S(1)}, s32[128]{0:T(128)}, u32[]{:S(2)}) copy-start(s32[128]{0:T(128)} %param.8) | copy-start | bytes 1540
Sparse Core Ops, SparseCore 0:
  17.6 40.5 all-gather.1
  318.4 67.9 reduce-scatter.1
where the time goes:
time: 396 us; the launch traced here: 395 us
  waiting for transfers between devices  304 us (77%)
  matrix products  24.7 us (6%)
  local copies, waits for them, and re-layouts  15.9 us (4%)
  starting transfers between devices  14.4 us (4%)
  other arithmetic  13.8 us (3%)
  between operations  13.6 us (3%)
  blocking collectives  8.4 us (2%)
    all_to_all x1, waiting for transfers between devices, body(): lax.all_to_all(sent_terms, 'tile', split_axis=1, concat_axis=1, tiled=True)  135 us
    all_to_all x1, waiting for transfers between devices, body(): lax.all_to_all(reply_rows, 'tile', split_axis=1, concat_axis=1, tiled=True)  70.8 us
    reduce_scatter x1, waiting for transfers between devices, body(): lax.psum_scatter(jnp.einsum('ct,mtk->cmk', picked, backward_terms, precis...  68.2 us
    all_gather x1, waiting for transfers between devices, body(): gathered = lax.all_gather(member_deviations, 'tile', axis=1, tiled=True)  30 us
    psum x1, blocking collectives, body(): ensemble_sum = lax.psum(local_sum, 'mem')  8.4 us
    dot_general x1, matrix products, body(): jnp.einsum('ds,msk->mdk', row_match, got_terms, precision=lax.Precision.H...  8.12 us
  transfers between devices with their start and end apart: 5, of which 4 were waited for; matrix products, arithmetic and copies ran while one was open for 7% of the time, Pallas kernels for 0%

commit v1 on v0

--- a/solution.py
+++ b/solution.py
@@ -61,7 +61,10 @@
     obs_weight = (precision_weight.astype(jnp.float32) / 8.0).reshape(SOUND_DEV, tile_size)
     weighted = (obs_weight[None, :, :] * (modelled - targets)).astype(jnp.bfloat16)
     reply_rows = jnp.take(weighted, jnp.minimum(got_rows, SOUND_DEV - 1), axis=1)
-    returned = lax.all_to_all(reply_rows, "tile", split_axis=1, concat_axis=1, tiled=True)
+    size = lax.axis_size("tile")
+    blocks = jnp.stack(jnp.split(reply_rows, size, axis=1), axis=0)
+    blocks = lax.all_to_all(blocks, "tile", split_axis=0, concat_axis=0)
+    returned = jnp.concatenate(blocks, axis=1)
     residual_tiles = jnp.take(returned, row_slot, axis=1)
     backward_terms = jnp.einsum(
         "mtr,trk->mtk", residual_tiles, footprints, preferred_element_type=jnp.float32

time: 396 us -> 401 us (1.013)
  local copies, waits for them, and re-layouts: 15.9 us -> 22.2 us
    unnamed x8 -> x15, local copies, waits for them, and re-layouts: 1.81 us -> 7.25 us
where the time goes in v1:
time: 401 us; the launch traced here: 400 us
  waiting for transfers between devices  304 us (76%)
  matrix products  24.7 us (6%)
  local copies, waits for them, and re-layouts  22.2 us (6%)
  starting transfers between devices  14.8 us (4%)
  between operations  13.6 us (3%)
  other arithmetic  12.5 us (3%)
  blocking collectives  8.4 us (2%)
    all_to_all x1, waiting for transfers between devices, body(): lax.all_to_all(sent_terms, 'tile', split_axis=1, concat_axis=1, tiled=True)  135 us
    all_to_all x1, waiting for transfers between devices, body(): blocks = lax.all_to_all(blocks, 'tile', split_axis=0, concat_axis=0)  70.6 us
    reduce_scatter x1, waiting for transfers between devices, body(): lax.psum_scatter(jnp.einsum('ct,mtk->cmk', picked, backward_terms, precis...  68.3 us
    all_gather x1, waiting for transfers between devices, body(): gathered = lax.all_gather(member_deviations, 'tile', axis=1, tiled=True)  30 us
    psum x1, blocking collectives, body(): ensemble_sum = lax.psum(local_sum, 'mem')  8.4 us
    dot_general x1, matrix products, body(): jnp.einsum('ds,msk->mdk', row_match, got_terms, precision=lax.Precision.H...  8.12 us
  transfers between devices with their start and end apart: 5, of which 4 were waited for; matrix products, arithmetic and copies ran while one was open for 7% of the time, Pallas kernels for 0%

profile of v1, /device:TPU:0, one launch (start us, length us, event | category | flops | bytes accessed | tf_op | source)
XLA Modules:
  0.0 400.1 jit_solution(11962337496920211988)
XLA Ops:
  6.5 0.0 all-gather.2.cloned.1.call-start
  6.5 0.9 convert_reduce_fusion
  7.5 8.4 %psum.7 = f32[1024]{0:T(1024)S(1)} all-reduce(f32[1024]{0:T(1024)S(1)} %convert_reduce_fusion), channel_id=1, replica_groups=mesh['tile'=8,'mem'=4] {'mem'}, use_global_device_ids=true, to_apply=%region_4.5 | all-reduce | flops 1024 | bytes 8192 | tf_op jit(solution)/shard_map/psum | solution.py:37
  15.9 1.6 fusion.32
  17.5 0.0 all-gather.2.cloned.1.call-update
  17.5 0.7 and_select_fusion
  18.2 0.2 convert_reduce_fusion.1
  18.4 0.1 select_reduce_fusion
  18.5 0.1 reduce_sum.33
  18.6 1.6 gather_fusion
  20.1 0.1 gather.23
  20.2 0.1 fusion.33
  20.3 0.1 reduce_or.12
  20.4 0.6 select_select_fusion
  21.0 5.8 %all-to-all-start = ((s32[1,8,24]{2,0,1:T(1,128)}), s32[1,8,24]{2,0,1:T(1,128)S(1)}, u32[]{:S(2)}, u32[]{:S(2)}) async-start(s32[1,8,24]{2,0,1:T(1,128)} %bitcast.3), calls=%async_computation | async-start | bytes 8192 | tf_op jit(solution)/shard_map/all_to_all | solution.py:55
  26.8 0.7 compare_select_fusion.5
  27.5 0.7 compare_and_fusion
  28.2 30.0 %all-gather.2.cloned.1.call-done = bf16[64,8192]{1,0:T(8,128)(2,1)} async-done(((bf16[64,1024]{1,0:T(8,128)(2,1)}), bf16[64,8192]{1,0:T(8,128)(2,1)}) %all-gather.2.cloned.1.call-update) | async-done | bytes 1048592 | tf_op jit(solution)/shard_map/all_gather | solution.py:46
  58.2 1.5 copy_bitcast_fusion
  59.7 1.0 gather_fusion.1
  60.7 7.0 %convolution_bitcast_fusion.1 = f32[64,128,128]{2,0,1:T(8,128)} fusion(bf16[128,128,128]{2,1,0:T(8,128)(2,1)} %param.6, bf16[128,64,128]{2,1,0:T(8,128)(2,1)S(1)} %gather_fusion.1, pred[128]{0:T(512)(128)(4,1)S(1)} %compare_and_fusion), kind=kOutput, calls=%fused_computation.12 | convolution fusion | flops 269484032 | bytes 10485888 | tf_op jit(solution)/shard_map/mtk,trk->mtr/dot_general | solution.py:48
  67.7 5.8 %gather_fusion.2 = f32[192,64,128]{2,1,0:T(8,128)} fusion(f32[64,128,128]{2,0,1:T(8,128)} %convolution_bitcast_fusion.1, s32[1024]{0:T(1024)S(1)} %pad_clamp_fusion.3), kind=kCustom, calls=%fused_computation.2 | custom fusion | bytes 12583680 | tf_op jit(solution)/shard_map/jit(_take)/gather | solution.py:25
  73.5 5.4 %select_bitcast_fusion = f32[64,192,128]{2,0,1:T(8,128)} fusion(f32[192,64,128]{2,1,0:T(8,128)} %gather_fusion.2, pred[192]{0:T(512)(128)(4,1)S(1)} %fusion.33, pred[192]{0:T(512)(128)(4,1)S(1)} %compare_and_fusion.1), kind=kLoop, calls=%fused_computation.7 | loop fusion | flops 3145728 | bytes 12583296 | tf_op jit(solution)/shard_map/jit(_where)/select_n | solution.py:26
  79.0 0.0 copy-start
  79.0 0.0 copy-start.1
  79.0 0.0 all-to-all-done
  79.0 5.1 %all-to-all-start.1 = ((f32[64,192,128]{2,0,1:T(8,128)}), f32[64,192,128]{2,0,1:T(8,128)}, u32[]{:S(2)}, u32[]{:S(2)}) async-start(f32[64,192,128]{2,0,1:T(8,128)} %select_bitcast_fusion), calls=%async_computation.1 | async-start | bytes 12582912 | tf_op jit(solution)/shard_map/all_to_all | solution.py:54
  84.0 0.0 copy-done
  84.0 0.1 copy.39
  84.1 0.0 copy-done.1
  84.2 0.5 broadcast.213
  84.7 0.7 minimum_reduce_fusion
  85.4 0.1 squeeze.3
  85.4 0.1 min.26
  85.6 135.0 %all-to-all-done.1 = f32[64,192,128]{2,0,1:T(8,128)} async-done(((f32[64,192,128]{2,0,1:T(8,128)}), f32[64,192,128]{2,0,1:T(8,128)}, u32[]{:S(2)}, u32[]{:S(2)}) %all-to-all-start.1) | async-done | bytes 6291488 | tf_op jit(solution)/shard_map/all_to_all | solution.py:54
  220.6 8.1 %fusion.19 = bf16[64,16,128]{2,1,0:T(8,128)(2,1)S(1)} fusion(f32[64,16,128]{2,1,0:T(8,128)S(1)} %bitcast.85, f32[64,192,128]{2,0,1:T(8,128)} %all-to-all-done.1, f32[16,128]{1,0:T(8,128)S(1)} %multiply_bitcast_fusion, s32[192]{0:T(256)S(1)} %squeeze.3), kind=kOutput, calls=%fused_computation.22 | convolution fusion | flops 302386176 | bytes 7086848 | tf_op jit(solution)/shard_map/ds,msk->mdk/dot_general | solution.py:59
  228.7 0.1 copy.33
  228.7 1.2 gather_fusion.3
  229.9 0.8 select_bitcast_fusion.1
  230.7 0.8 fusion.31
  231.5 0.8 fusion.30
  232.3 0.8 fusion.29
  233.0 0.8 fusion.28
  233.8 0.8 fusion.27
  234.6 0.8 fusion.26
  235.4 0.8 fusion.25
  236.2 0.8 fusion.24
  236.9 3.6 all-to-all-start.2
  240.6 0.3 reduce-scatter.2.cloned.1.call-start
  240.9 70.6 %all-to-all-done.2 = bf16[8,64,24,128]{3,1,2,0:T(8,128)(2,1)S(1)} async-done(((bf16[8,64,24,128]{3,1,2,0:T(8,128)(2,1)}), bf16[8,64,24,128]{3,1,2,0:T(8,128)(2,1)S(1)}, u32[]{:S(2)}, u32[]{:S(2)}) %all-to-all-start.2) | async-done | bytes 3145760 | tf_op jit(solution)/shard_map/all_to_all | solution.py:66
  311.5 2.2 gather_fusion.4
  313.6 0.0 copy-start.2
  313.6 4.1 %convolution_bitcast_fusion = f32[64,128,128]{2,0,1:T(8,128)S(1)} fusion(bf16[128,128,128]{2,1,0:T(8,128)(2,1)} %param.6, bf16[128,64,128]{2,1,0:T(8,128)(2,1)} %gather_fusion.4, pred[128]{0:T(512)(128)(4,1)S(1)} %get-tuple-element.7), kind=kOutput, calls=%fused_computation.11 | convolution fusion | flops 269484032 | bytes 10485888 | tf_op jit(solution)/shard_map/mtr,trk->mtk/dot_general | solution.py:69
  317.7 0.0 copy-done.2
  317.7 5.5 %fusion.2 = f32[64,64,128]{2,0,1:T(8,128)} fusion(f32[64,128,128]{2,0,1:T(8,128)S(1)} %convolution_bitcast_fusion, s32[128]{0:T(128)S(1)} %copy-done.2), kind=kOutput, calls=%fused_computation.8 | convolution fusion | flops 805314560 | bytes 6291968 | tf_op jit(solution)/shard_map/ct,mtk->cmk/dot_general | solution.py:76
  323.2 0.0 reduce-scatter.2.cloned.1.call-update
  323.2 68.3 %reduce-scatter.2.cloned.1.call-done = f32[8,64,128]{2,0,1:T(8,128)} async-done(((f32[64,64,128]{2,0,1:T(8,128)}), f32[8,64,128]{2,0,1:T(8,128)}) %reduce-scatter.2.cloned.1.call-update) | async-done | bytes 262160 | tf_op jit(solution)/shard_map/reduce_scatter | solution.py:75
  391.6 1.7 copy.55
  (12 shorter events, 0.1 us)
Async XLA Ops:
  6.5 51.7 %all-gather.2.cloned.1.call-start = ((), (), s32[]{:S(2)}) async-start(), calls=%async_computation.4 | async-start | bytes 1179648 | tf_op jit(solution)/shard_map/all_gather | solution.py:46
  21.0 57.9 %all-to-all-start = ((s32[1,8,24]{2,0,1:T(1,128)}), s32[1,8,24]{2,0,1:T(1,128)S(1)}, u32[]{:S(2)}, u32[]{:S(2)}) async-start(s32[1,8,24]{2,0,1:T(1,128)} %bitcast.3), calls=%async_computation | async-start | bytes 8192 | tf_op jit(solution)/shard_map/all_to_all | solution.py:55
  79.0 5.1 %copy-start = (f32[64,2048]{1,0:T(8,128)S(1)}, f32[64,2048]{1,0:T(8,128)}, u32[]{:S(2)}) copy-start(f32[64,2048]{1,0:T(8,128)} %param.10) | copy-start | bytes 1572868
  79.0 5.2 %copy-start.1 = (s32[2048]{0:T(1024)S(1)}, s32[2048]{0:T(1024)}, u32[]{:S(2)}) copy-start(s32[2048]{0:T(1024)} %param.11) | copy-start | bytes 24580
  79.0 141.6 %all-to-all-start.1 = ((f32[64,192,128]{2,0,1:T(8,128)}), f32[64,192,128]{2,0,1:T(8,128)}, u32[]{:S(2)}, u32[]{:S(2)}) async-start(f32[64,192,128]{2,0,1:T(8,128)} %select_bitcast_fusion), calls=%async_computation.1 | async-start | bytes 12582912 | tf_op jit(solution)/shard_map/all_to_all | solution.py:54
  236.9 74.5 %all-to-all-start.2 = ((bf16[8,64,24,128]{3,1,2,0:T(8,128)(2,1)}), bf16[8,64,24,128]{3,1,2,0:T(8,128)(2,1)S(1)}, u32[]{:S(2)}, u32[]{:S(2)}) async-start(bf16[8,64,24,128]{3,1,2,0:T(8,128)(2,1)} %fusion.24), calls=%async_computation.2 | async-start | bytes 6291456 | tf_op jit(solution)/shard_map/all_to_all | solution.py:66
  240.6 151.0 %reduce-scatter.2.cloned.1.call-start = ((), (), s32[]{:S(2)}) async-start(), calls=%async_computation.5 | async-start | bytes 2359296 | tf_op jit(solution)/shard_map/reduce_scatter | solution.py:75
  313.6 4.1 %copy-start.2 = (s32[128]{0:T(128)S(1)}, s32[128]{0:T(128)}, u32[]{:S(2)}) copy-start(s32[128]{0:T(128)} %param.8) | copy-start | bytes 1540
Sparse Core Ops, SparseCore 0:
  17.6 40.5 all-gather.1
  323.3 68.1 reduce-scatter.1
